TPU v7x, 64 devices: a 2x2x8 block of a 4x4x8 slice. The times are simulated.
64 devices in a mesh: dp: 4 (over x, y), wg: 16 (over z, core).
Axes of the slice: x: 2, y: 2, z: 8, core: 2. Of those that a mesh axis runs over, the one named last changes fastest.
The devices are a block of a 4x4x8 slice.
Arguments:
- hidden: bfloat16 [65536, 1024], P(('dp', 'wg')), parts along dimension 0
- choice: int32 [65536, 8], P(('dp', 'wg')), parts along dimension 0
- pre_scale: float32 [1024], replicated
- w_router: bfloat16 [1024, 32], replicated
- w_gelu: bfloat16 [32, 1024, 512], P(None, None, 'wg')
- w_linear: bfloat16 [32, 1024, 512], P(None, None, 'wg')
- w_down: bfloat16 [32, 512, 1024], P(None, 'wg')
- post_scale: float32 [1024], replicated
Outputs:
- output: bfloat16 [65536, 1024], P(('dp', 'wg')), parts along dimension 0
There are 4 independent parts. A program takes and returns all parts, laid end to end along the dimension named above; an argument that names none is the same for every part.
All inputs are finite; a program needn't handle non-finite values.
Results may differ from a plain program's by a relative error of at most 0.001.
Values are sent between devices in bfloat16 or wider.
A program may use at most 768 MiB of HBM per device.

v0:
```python
import functools
import math

import jax
import jax.numpy as jnp
from jax import lax
from jax.experimental import pallas as pl
from jax.experimental.pallas import tpu as pltpu
from jax.sharding import PartitionSpec as P

EPS = 1e-5
MESH = pl.DeviceIdType.MESH
SUB = 256
VMEM_BYTES = 67_043_328
OUT = 2 << 20


def dot_t(lhs, rhs):
    return lax.dot_general(lhs, rhs, (((1,), (1,)), ((), ())), preferred_element_type=jnp.float32)


def exclusive_experts(experts):
    count = experts * 11 // 32
    while (experts - count) % 3:
        count -= 1
    return count


def moe_kernel(side, chips, excl, hid_ref, choice_ref, pre_ref, post_ref, router_ref, wg_ref, wl_ref, wd_ref, out_ref,
               wts, rows, acc, gate_t, gates, tmp, up_ss, up_rs, dn_ss, dn_rs, y_ss, y_rs, load_sem, row_ss, row_rs, gate_ss, gate_rs,
               fold_ss, fold_rs, cross_ss, cross_rs, part_ss, part_rs, freed, credit):
    tok, d_model = hid_ref.shape
    held, _, _, shard, _ = wts.shape
    experts = held + excl
    width = chips * shard
    slots = chips - 1
    rounds = held // 3
    count = rounds * slots
    ncol = min(256, d_model)
    chunks = 4
    chunk = tok // chunks
    sub = min(SUB, tok)

    dp, wg = lax.axis_index('dp'), lax.axis_index('wg')
    z, core = wg // 2, wg % 2
    gx, gy = dp // side, dp % side
    px, py = gx % 2, gy % 2
    up = (dp, ((z + 1) % chips) * 2 + core)
    down = (dp, ((z + chips - 1) % chips) * 2 + core)
    sib = (dp, wg + 1 - 2 * core)
    cross = (dp + side * (1 - 2 * px), wg)
    along = (dp + 1 - 2 * py, wg)

    def remote(src, dst, ss, rs, where):
        return pltpu.make_async_remote_copy(src_ref=src, dst_ref=dst, send_sem=ss, recv_sem=rs, device_id=where, device_id_type=MESH)

    def slice_copy(i, chip, ss, rs, m, where):
        ref = wts.at[i, chip]
        return remote(ref, ref, ss.at[m], rs.at[m], where)

    def up_copy(m, back):
        r, j = m // slots, m % slots
        odd, s = j % 2, j // 2 + 1
        i = 3 * r + (1 - odd) * 2 * py + odd
        return slice_copy(i, (z - s + back + chips) % chips, up_ss, up_rs, m, up)

    def dn_copy(m, back):
        r, j = m // slots, m % slots
        odd, s = j % 2, j // 2 + 1
        i = 3 * r + odd * 2 * py + (1 - odd)
        return slice_copy(i, (z + s - back) % chips, dn_ss, dn_rs, m, down)

    def y_copy(m, i):
        r, j = m // slots, m % slots
        odd, s = j % 2, j // 2 + 1
        return slice_copy(3 * r + i, (z + (2 * odd - 1) * s + chips) % chips, y_ss, y_rs, m, along)

    def exchange(m, more=True):
        up_copy(m, 0).wait_recv()
        if more is True:
            up_copy(m + 2, 1).start()
        else:
            pl.when(m + 2 < count)(lambda: up_copy(m + 2, 1).start())
        dn_copy(m, 0).wait_recv()
        if more is True:
            dn_copy(m + 2, 1).start()
        else:
            pl.when(m + 2 < count)(lambda: dn_copy(m + 2, 1).start())
        y_copy(m, 2 * py).start()

    def partner_slices(r):
        @pl.loop(0, slots)
        def _(k):
            y_copy(r * slots + k, 2 - 2 * py).wait_recv()

    def row_copy(k, where):
        return remote(rows.at[0] if k < 3 else rows.at[2], rows.at[k], row_ss.at[k - 1], row_rs.at[k - 1], where)

    def gate_copy(k, where):
        return remote(gate_t.at[0] if k < 3 else gate_t.at[2], gate_t.at[k], gate_ss.at[k - 1], gate_rs.at[k - 1], where)

    def part_of(c):
        return pl.ds(pl.multiple_of(c * chunk, chunk), chunk)

    def fold_copy(c):
        return remote(acc.at[3, part_of(c)], tmp.at[c % 2], fold_ss.at[c], fold_rs.at[c], sib)

    def cross_copy(c):
        return remote(acc.at[2, part_of(c)], tmp.at[(c + 2) % 3], cross_ss.at[c], cross_rs.at[c], cross)

    def free(sem, where):
        pl.semaphore_signal(sem, inc=1, device_id=where, device_id_type=MESH)

    def last_copy(c):
        at = part_of(c)
        return remote(acc.at[1, at], acc.at[3, at], part_ss.at[c], part_rs.at[c], sib)

    loads = []
    for n, (src0, dst0, size) in enumerate(((px * excl, 0, 3), (px * excl + 3, 3, excl - 3), (2 * excl, excl, held - excl))):
        for k, src in enumerate((wg_ref, wl_ref, wd_ref)):
            loads.append(pltpu.make_async_copy(src.at[pl.ds(src0, size)], wts.at[pl.ds(dst0, size), z, k], load_sem.at[3 * n + k]))
    hid_load = pltpu.make_async_copy(hid_ref, rows.at[0], load_sem.at[9])
    for load in loads[:3] + [hid_load] + loads[3:]:
        load.start()

    barrier = pltpu.get_barrier_semaphore()
    for peer in (up, down, sib, cross, along):
        pl.semaphore_signal(barrier, inc=1, device_id=peer, device_id_type=MESH)
    pl.semaphore_wait(barrier, 5)

    for load in loads[:3]:
        load.wait()
    for m in range(2):
        up_copy(m, 1).start()
        dn_copy(m, 1).start()

    hid_load.wait()
    nrm = min(128, chunk)

    @pl.loop(0, tok // nrm)
    def _(i):
        at = pl.ds(pl.multiple_of(i * nrm, nrm), nrm)
        values = rows[0, at, :].astype(jnp.float32)
        scale = lax.rsqrt(jnp.mean(values * values, axis=-1, keepdims=True) + EPS)
        rows[0, at, :] = (values * scale * pre_ref[...]).astype(jnp.bfloat16)

    for load in loads[3:]:
        load.wait()

    rtr = min(256, tok)

    @pl.loop(0, tok // rtr)
    def _(i):
        at = pl.ds(pl.multiple_of(i * rtr, rtr), rtr)
        logits = dot_t(router_ref[...], rows[0, at, :])
        shifted = jnp.exp(logits - jnp.max(logits, axis=0, keepdims=True))
        probs = shifted / jnp.sum(shifted, axis=0, keepdims=True)
        expert_ids = lax.broadcasted_iota(jnp.int32, (experts, rtr), 0)
        picks = choice_ref[:, at]
        chosen = expert_ids == picks[0:1, :]
        for j in range(1, picks.shape[0]):
            chosen = chosen | (expert_ids == picks[j:j + 1, :])
        gate_t[0, :, at] = jnp.where(chosen, probs, -1.0)

    @pl.loop(0, 4 * tok // nrm)
    def _(i):
        at = pl.ds(pl.multiple_of((i // 4) * nrm, nrm), nrm)
        acc[i % 4, at, :] = jnp.zeros((nrm, d_model), jnp.float32)

    for k, where in ((2, cross), (1, sib)):
        gate_copy(k, where).start()
        row_copy(k, where).start()

    def spread_gates(k):
        gates[:, k * experts:(k + 1) * experts] = gate_t[k].T

    spread_gates(0)

    @pl.loop(0, slots)
    def _(j):
        exchange(j)

    row_copy(1, sib).wait_recv()
    gate_copy(1, sib).wait_recv()
    spread_gates(1)

    def work(i, k, starts, size):
        e = i + excl * (px + (1 - px) * jnp.minimum(i // excl, 1)) + k * experts
        lane = lax.broadcasted_iota(jnp.int32, (size, 4 * experts), 1)
        c = math.sqrt(2.0 / math.pi)
        acts = []
        for start in starts:
            at = pl.ds(pl.multiple_of(start, size), size)
            x = rows[k, at, :]
            u = dot_t(x, wts[i, :, 0].reshape(width, d_model))
            v = dot_t(x, wts[i, :, 1].reshape(width, d_model))
            gate = jnp.sum(jnp.where(lane == e, gates[at, :], 0.0), axis=1, keepdims=True)
            cdf = 0.5 * (1.0 + jnp.tanh(c * (u + 0.044715 * (u * u * u))))
            acts.append((at, gate, jnp.where(gate >= 0.0, u * cdf * v, 0.0).astype(jnp.bfloat16)))
        for at, gate, a in acts:
            for n in range(d_model // ncol):
                cols = pl.ds(n * ncol, ncol)
                o = jnp.dot(a, wts[i, :, 2, :, cols].reshape(width, ncol), preferred_element_type=jnp.float32)
                acc[k, at, cols] += gate * o

    def unit(i, k):
        work(i, k, [n * sub for n in range(tok // sub)], sub)

    def held_index(r, w):
        return 3 * r + w + (1 - w) * 2 * py

    def triple(r, q, sets):
        unit(held_index(r, q // 2), sets + q % 2)

    def run(m0, m1, units, one, actions=(), more=True):
        span = m1 - m0

        @pl.loop(0, span)
        def _(j):
            exchange(m0 + j, more)
            for slot, action in actions:
                pl.when(j == slot)(action)

            @pl.loop((units * j + span - 1) // span, (units * (j + 1) + span - 1) // span)
            def _(q):
                one(q)

    run(slots, 2 * slots, 6, lambda q: triple(0, q, 0), [(4, lambda: partner_slices(0))])

    row_copy(2, cross).wait_recv()
    gate_copy(2, cross).wait_recv()
    row_copy(3, sib).start()
    gate_copy(3, sib).start()
    spread_gates(2)

    def far_rows():
        row_copy(3, sib).wait_recv()
        gate_copy(3, sib).wait_recv()
        spread_gates(3)

    run(2 * slots, 3 * slots, 12, lambda q: triple(1 - q // 6, q % 6, 2 * (q // 6)), [(2, lambda: partner_slices(1)), (4, far_rows)])
    run(3 * slots, 4 * slots - 1, 12, lambda q: triple(1 + q // 6, q % 6, 2), [(5, lambda: partner_slices(2))])
    m = 4 * slots - 1
    exchange(m)

    pl.loop(0, 2)(lambda q: unit(excl - 1, 3 - q))
    exchange(m + 1)
    partner_slices(3)

    def late(k, c):
        work(excl - 2, k, [c * chunk], chunk)

    def fold_in(c, slot):
        fold_copy(c).wait_recv()
        acc[2, part_of(c), :] += tmp[slot]

    @pl.loop(0, 2)
    def _(c):
        late(3, c)
        fold_copy(c).start()
        late(2, c)

    exchange(m + 2)

    @pl.loop(0, 2)
    def _(c):
        late(3, 2 + c)
        late(2, 2 + c)
        fold_in(c, c)
        free(freed.at[c], sib)
        pl.when(c == 0)(lambda: cross_copy(0).start())

    for c in range(2):
        pl.semaphore_wait(freed.at[c], 1)
        fold_copy(2 + c).start()
    exchange(m + 3)
    for c in range(2):
        fold_in(2 + c, c)
        free(credit.at[c], cross)
    for c in range(2):
        pl.semaphore_wait(credit.at[c], 1)
        cross_copy(1 + c).start()
    pl.loop(0, chunks)(lambda c: fold_copy(c).wait_send())
    free(freed.at[2], sib)

    def first_sums():
        cross_copy(0).wait_recv()
        acc[0, part_of(0), :] += tmp[2]
        free(credit.at[2], cross)

    def last_sums():
        pl.semaphore_wait(credit.at[2], 1)
        cross_copy(3).start()

    run(m + 4, 5 * slots, 6, lambda q: triple(2, q, 0))
    row_copy(3, sib).wait_send()
    hid_again = pltpu.make_async_copy(hid_ref, rows.at[3], load_sem.at[9])
    hid_again.start()
    run(5 * slots, 6 * slots, 12, lambda q: triple(3 + q // 6, q % 6, 0), [(4, first_sums), (5, lambda: partner_slices(4)), (6, last_sums)])
    run(6 * slots, 7 * slots - 1, 6, lambda q: triple(5, q, 0), [(4, lambda: partner_slices(5))], more=False)
    exchange(count - 1, more=None)

    last = rounds - 1
    pl.loop(0, 3)(lambda q: unit(held_index(last, q % 2), 1 - q // 2))
    partner_slices(last)
    pl.semaphore_wait(freed.at[2], 1)

    @pl.loop(0, chunks)
    def _(c):
        work(held_index(last, 2), 1, [c * chunk], chunk)
        last_copy(c).start()

    pl.loop(1, 3)(lambda q: unit(held_index(last, q), 0))

    @pl.loop(0, count)
    def _(m):
        up_copy(m, 1).wait_send()
        dn_copy(m, 1).wait_send()
        y_copy(m, 2 * py).wait_send()

    for k, where in ((1, sib), (2, cross)):
        row_copy(k, where).wait_send()
    for k, where in ((1, sib), (2, cross), (3, sib)):
        gate_copy(k, where).wait_send()
    hid_again.wait()

    for c in range(chunks):
        last_copy(c).wait()
        cross_copy(c).wait_send()
        if c:
            cross_copy(c).wait_recv()

        @pl.loop(0, chunk // nrm)
        def _(i):
            at = pl.ds(pl.multiple_of(c * chunk + i * nrm, nrm), nrm)
            mixed = acc[0, at, :] + acc[3, at, :]
            if c:
                mixed += tmp[(c + 2) % 3, pl.ds(pl.multiple_of(i * nrm, nrm), nrm), :]
            scale = lax.rsqrt(jnp.mean(mixed * mixed, axis=-1, keepdims=True) + EPS)
            out_ref[at, :] = (rows[3, at, :].astype(jnp.float32) + mixed * scale * post_ref[...]).astype(jnp.bfloat16)


def write_kernel(src_ref, dst_ref, sem):
    write = pltpu.make_async_copy(src_ref, dst_ref, sem)
    write.start()
    write.wait()


def solution(mesh):
    side = math.isqrt(mesh.shape['dp'])
    chips = mesh.shape['wg'] // 2

    def local_block(hidden, choice, pre_scale, w_router, w_gelu, w_linear, w_down, post_scale):
        tok, d_model = hidden.shape
        experts, _, shard = w_gelu.shape
        excl = exclusive_experts(experts)
        held = experts - excl
        count = (held // 3) * (chips - 1)
        dma = pltpu.SemaphoreType.DMA
        vmem = pl.BlockSpec(memory_space=pltpu.VMEM)
        any_space = pl.BlockSpec(memory_space=pl.ANY)
        flops = 2 * 2 * tok * experts * 3 * (chips * shard) * d_model
        out = pl.pallas_call(
            functools.partial(moe_kernel, side, chips, excl),
            out_shape=pltpu.VMEM((tok, d_model), jnp.bfloat16),
            in_specs=[any_space, vmem, vmem, vmem, vmem, any_space, any_space, any_space],
            out_specs=vmem,
            scratch_shapes=[
                pltpu.VMEM((held, chips, 3, shard, d_model), jnp.bfloat16),
                pltpu.VMEM((4, tok, d_model), jnp.bfloat16),
                pltpu.VMEM((4, tok, d_model), jnp.float32),
                pltpu.VMEM((4, experts, tok), jnp.float32),
                pltpu.VMEM((tok, 4 * experts), jnp.float32),
                pltpu.VMEM((3, tok // 4, d_model), jnp.float32),
                dma((count,)), dma((count,)), dma((count,)), dma((count,)), dma((count,)), dma((count,)),
                dma((10,)),
                dma((3,)), dma((3,)), dma((3,)), dma((3,)),
                dma((4,)), dma((4,)), dma((4,)), dma((4,)), dma((4,)), dma((4,)),
                pltpu.SemaphoreType.REGULAR((3,)), pltpu.SemaphoreType.REGULAR((3,)),
            ],
            compiler_params=pltpu.CompilerParams(collective_id=0, has_side_effects=True, vmem_limit_bytes=VMEM_BYTES - OUT),
            cost_estimate=pl.CostEstimate(flops=flops, bytes_accessed=8 * experts * chips * shard * d_model, transcendentals=0),
        )(hidden, choice.T, pre_scale.reshape(1, d_model), post_scale.reshape(1, d_model), w_router.T, jnp.swapaxes(w_gelu, 1, 2), jnp.swapaxes(w_linear, 1, 2), w_down)

        return pl.pallas_call(
            write_kernel,
            out_shape=jax.ShapeDtypeStruct((tok, d_model), jnp.bfloat16),
            in_specs=[vmem],
            out_specs=any_space,
            scratch_shapes=[dma(())],
        )(pltpu.with_memory_space_constraint(out, pltpu.VMEM))

    row_spec = P(('dp', 'wg'), None)
    weight_in = P(None, None, 'wg')
    return jax.shard_map(local_block, mesh=mesh, in_specs=(row_spec, row_spec, P(), P(), weight_in, weight_in, P(None, 'wg', None), P()), out_specs=row_spec, check_vma=False)
```

profile of v0, /device:TPU:21, one launch (start us, length us, event | category | flops | bytes accessed | tf_op | source)
XLA Modules:
  0.0 238.0 jit_solution(1843393966903764521)
XLA Ops:
  0.0 236.5 %shard_map.82.src_ref = bf16[1024,1024]{1,0:T(8,128)(2,1)S(1)} custom-call(bf16[1024,1024]{1,0:T(8,128)(2,1)} %hid_ref.1, s32[8,1024]{1,0:T(8,128)} %bitcast.9, f32[1,1024]{1,0:T(1,128)} %bitcast.10, f32[1,1024]{1,0:T(1,128)} %bitcast.11, bf16[32,1024]{1,0:T(8,128)(2,1)} %bitcast.8, bf16[32,32,1024]{2,1,0:T(8,128)(2,1)} %bitcast.6, ...), custom_call_target="tpu_custom_call" | custom-call | flops 103079215104 | bytes 67108864 | tf_op jit(solution)/shard_map/pallas_call | solution.py:363
  236.5 1.3 shard_map.83
where the time goes:
time: 238 us
  Pallas kernels  238 us (100%)
    pallas_call x1, Pallas kernels, local_block(): pl.pallas_call(functools.partial(moe_kernel, side, chips, excl), out_shap...  236 us

commit v1 on v0

--- a/solution.py
+++ b/solution.py
@@ -75,7 +75,7 @@
         odd, s = j % 2, j // 2 + 1
         return slice_copy(3 * r + i, (z + (2 * odd - 1) * s + chips) % chips, y_ss, y_rs, m, along)
 
-    def exchange(m, more=True):
+    def exchange(m, more=True, along_y=True):
         up_copy(m, 0).wait_recv()
         if more is True:
             up_copy(m + 2, 1).start()
@@ -86,12 +86,16 @@
             dn_copy(m + 2, 1).start()
         else:
             pl.when(m + 2 < count)(lambda: dn_copy(m + 2, 1).start())
-        y_copy(m, 2 * py).start()
-
-    def partner_slices(r):
-        @pl.loop(0, slots)
+        if along_y:
+            y_copy(m, 2 * py).start()
+
+    def partner_slices(r, first=0, end=slots):
+        @pl.loop(first, end)
         def _(k):
             y_copy(r * slots + k, 2 - 2 * py).wait_recv()
+
+    def far_copy(back):
+        return slice_copy(3 * (rounds - 1) + 2 - 2 * py, (z - chips // 2 + back + chips) % chips, up_ss, up_rs, count, up)
 
     def row_copy(k, where):
         return remote(rows.at[0] if k < 3 else rows.at[2], rows.at[k], row_ss.at[k - 1], row_rs.at[k - 1], where)
@@ -264,11 +268,11 @@
 
     @pl.loop(0, 2)
     def _(c):
-        late(3, 2 + c)
-        late(2, 2 + c)
         fold_in(c, c)
         free(freed.at[c], sib)
         pl.when(c == 0)(lambda: cross_copy(0).start())
+        late(3, 2 + c)
+        late(2, 2 + c)
 
     for c in range(2):
         pl.semaphore_wait(freed.at[c], 1)
@@ -298,11 +302,14 @@
     hid_again.start()
     run(5 * slots, 6 * slots, 12, lambda q: triple(3 + q // 6, q % 6, 0), [(4, first_sums), (5, lambda: partner_slices(4)), (6, last_sums)])
     run(6 * slots, 7 * slots - 1, 6, lambda q: triple(5, q, 0), [(4, lambda: partner_slices(5))], more=False)
-    exchange(count - 1, more=None)
-
     last = rounds - 1
-    pl.loop(0, 3)(lambda q: unit(held_index(last, q % 2), 1 - q // 2))
-    partner_slices(last)
+    partner_slices(last, 0, slots - 2)
+    far_copy(1).start()
+    exchange(count - 1, more=None, along_y=False)
+
+    pl.loop(0, 2)(lambda q: unit(held_index(last, q), 1))
+    partner_slices(last, slots - 2, slots - 1)
+    far_copy(0).wait_recv()
     pl.semaphore_wait(freed.at[2], 1)
 
     @pl.loop(0, chunks)
@@ -310,13 +317,15 @@
         work(held_index(last, 2), 1, [c * chunk], chunk)
         last_copy(c).start()
 
-    pl.loop(1, 3)(lambda q: unit(held_index(last, q), 0))
+    pl.loop(0, 3)(lambda q: unit(held_index(last, q), 0))
 
     @pl.loop(0, count)
     def _(m):
         up_copy(m, 1).wait_send()
         dn_copy(m, 1).wait_send()
-        y_copy(m, 2 * py).wait_send()
+        pl.when(m < count - 1)(lambda: y_copy(m, 2 * py).wait_send())
+
+    far_copy(1).wait_send()
 
     for k, where in ((1, sib), (2, cross)):
         row_copy(k, where).wait_send()
@@ -372,7 +381,7 @@
                 pltpu.VMEM((4, experts, tok), jnp.float32),
                 pltpu.VMEM((tok, 4 * experts), jnp.float32),
                 pltpu.VMEM((3, tok // 4, d_model), jnp.float32),
-                dma((count,)), dma((count,)), dma((count,)), dma((count,)), dma((count,)), dma((count,)),
+                dma((count + 1,)), dma((count + 1,)), dma((count,)), dma((count,)), dma((count,)), dma((count,)),
                 dma((10,)),
                 dma((3,)), dma((3,)), dma((3,)), dma((3,)),
                 dma((4,)), dma((4,)), dma((4,)), dma((4,)), dma((4,)), dma((4,)),

time: 238 us -> 238 us (level)
  no operation moved by 1% of the time
where the time goes in v1:
time: 238 us; the launch traced here: 237 us
  Pallas kernels  237 us (100%)
    pallas_call x1, Pallas kernels, local_block(): pl.pallas_call(functools.partial(moe_kernel, side, chips, excl), out_shap...  236 us

profile of v1, /device:TPU:21, one launch (start us, length us, event | category | flops | bytes accessed | tf_op | source)
XLA Modules:
  0.0 237.1 jit_solution(13455851161826022902)
XLA Ops:
  0.0 235.6 %shard_map.82.src_ref = bf16[1024,1024]{1,0:T(8,128)(2,1)S(1)} custom-call(bf16[1024,1024]{1,0:T(8,128)(2,1)} %hid_ref.1, s32[8,1024]{1,0:T(8,128)} %bitcast.9, f32[1,1024]{1,0:T(1,128)} %bitcast.10, f32[1,1024]{1,0:T(1,128)} %bitcast.11, bf16[32,1024]{1,0:T(8,128)(2,1)} %bitcast.8, bf16[32,32,1024]{2,1,0:T(8,128)(2,1)} %bitcast.6, ...), custom_call_target="tpu_custom_call" | custom-call | flops 103079215104 | bytes 67108864 | tf_op jit(solution)/shard_map/pallas_call | solution.py:372
  235.6 1.3 shard_map.83

commit v2 on v1

--- a/solution.py
+++ b/solution.py
@@ -106,11 +106,16 @@
     def part_of(c):
         return pl.ds(pl.multiple_of(c * chunk, chunk), chunk)
 
-    def fold_copy(c):
-        return remote(acc.at[3, part_of(c)], tmp.at[c % 2], fold_ss.at[c], fold_rs.at[c], sib)
-
-    def cross_copy(c):
-        return remote(acc.at[2, part_of(c)], tmp.at[(c + 2) % 3], cross_ss.at[c], cross_rs.at[c], cross)
+    h = chunk // 2
+    pieces = ((0, h, 0, 0, 2, 0), (h, h, 0, h, 2, h), (chunk, chunk, 1, 0, 0, 0), (2 * chunk, chunk, 0, 0, 1, 0), (3 * chunk, chunk, 1, 0, 2, 0))
+
+    def fold_copy(n):
+        at, size, slot, row, _, _ = pieces[n]
+        return remote(acc.at[3, pl.ds(at, size)], tmp.at[slot, pl.ds(row, size)], fold_ss.at[n], fold_rs.at[n], sib)
+
+    def cross_copy(n):
+        at, size, _, _, slot, row = pieces[n]
+        return remote(acc.at[2, pl.ds(at, size)], tmp.at[slot, pl.ds(row, size)], cross_ss.at[n], cross_rs.at[n], cross)
 
     def free(sem, where):
         pl.semaphore_signal(sem, inc=1, device_id=where, device_id_type=MESH)
@@ -124,7 +129,7 @@
         for k, src in enumerate((wg_ref, wl_ref, wd_ref)):
             loads.append(pltpu.make_async_copy(src.at[pl.ds(src0, size)], wts.at[pl.ds(dst0, size), z, k], load_sem.at[3 * n + k]))
     hid_load = pltpu.make_async_copy(hid_ref, rows.at[0], load_sem.at[9])
-    for load in loads[:3] + [hid_load] + loads[3:]:
+    for load in loads[:3]:
         load.start()
 
     barrier = pltpu.get_barrier_semaphore()
@@ -138,8 +143,17 @@
         up_copy(m, 1).start()
         dn_copy(m, 1).start()
 
+    router_load = pltpu.make_async_copy(router_ref, out_ref.at[pl.ds(0, experts)], load_sem.at[10])
+    for load in [hid_load, router_load] + loads[3:]:
+        load.start()
+    nrm = min(128, chunk)
+
+    @pl.loop(0, 4 * tok // nrm)
+    def _(i):
+        at = pl.ds(pl.multiple_of((i // 4) * nrm, nrm), nrm)
+        acc[i % 4, at, :] = jnp.zeros((nrm, d_model), jnp.float32)
+
     hid_load.wait()
-    nrm = min(128, chunk)
 
     @pl.loop(0, tok // nrm)
     def _(i):
@@ -151,12 +165,13 @@
     for load in loads[3:]:
         load.wait()
 
+    router_load.wait()
     rtr = min(256, tok)
 
     @pl.loop(0, tok // rtr)
     def _(i):
         at = pl.ds(pl.multiple_of(i * rtr, rtr), rtr)
-        logits = dot_t(router_ref[...], rows[0, at, :])
+        logits = dot_t(out_ref[pl.ds(0, experts), :], rows[0, at, :])
         shifted = jnp.exp(logits - jnp.max(logits, axis=0, keepdims=True))
         probs = shifted / jnp.sum(shifted, axis=0, keepdims=True)
         expert_ids = lax.broadcasted_iota(jnp.int32, (experts, rtr), 0)
@@ -165,11 +180,6 @@
         for j in range(1, picks.shape[0]):
             chosen = chosen | (expert_ids == picks[j:j + 1, :])
         gate_t[0, :, at] = jnp.where(chosen, probs, -1.0)
-
-    @pl.loop(0, 4 * tok // nrm)
-    def _(i):
-        at = pl.ds(pl.multiple_of((i // 4) * nrm, nrm), nrm)
-        acc[i % 4, at, :] = jnp.zeros((nrm, d_model), jnp.float32)
 
     for k, where in ((2, cross), (1, sib)):
         gate_copy(k, where).start()
@@ -251,50 +261,69 @@
     exchange(m + 1)
     partner_slices(3)
 
-    def late(k, c):
-        work(excl - 2, k, [c * chunk], chunk)
-
-    def fold_in(c, slot):
-        fold_copy(c).wait_recv()
-        acc[2, part_of(c), :] += tmp[slot]
+    def late(k, start, size):
+        work(excl - 2, k, [start], size)
+
+    def fold_in(n):
+        at, size, slot, row, _, _ = pieces[n]
+        fold_copy(n).wait_recv()
+
+        @pl.loop(0, size // h)
+        def _(i):
+            acc[2, pl.ds(pl.multiple_of(at + i * h, h), h), :] += tmp[slot, pl.ds(pl.multiple_of(row + i * h, h), h), :]
 
     @pl.loop(0, 2)
+    def _(n):
+        late(3, n * h, h)
+        part = pl.ds(pl.multiple_of(n * h, h), h)
+        remote(acc.at[3, part], tmp.at[0, part], fold_ss.at[n], fold_rs.at[n], sib).start()
+        late(2, n * h, h)
+
+    late(3, *pieces[2][:2])
+    fold_copy(2).start()
+    fold_in(0)
+    cross_copy(0).start()
+    exchange(m + 2)
+    late(2, *pieces[2][:2])
+    fold_in(1)
+    cross_copy(1).start()
+    free(freed.at[0], sib)
+    fold_in(2)
+    free(freed.at[1], sib)
+
+    @pl.loop(2, chunks)
     def _(c):
-        late(3, c)
-        fold_copy(c).start()
-        late(2, c)
-
-    exchange(m + 2)
-
-    @pl.loop(0, 2)
-    def _(c):
-        fold_in(c, c)
-        free(freed.at[c], sib)
-        pl.when(c == 0)(lambda: cross_copy(0).start())
-        late(3, 2 + c)
-        late(2, 2 + c)
-
-    for c in range(2):
-        pl.semaphore_wait(freed.at[c], 1)
-        fold_copy(2 + c).start()
+        late(3, c * chunk, chunk)
+        late(2, c * chunk, chunk)
+
+    for n in range(2):
+        pl.semaphore_wait(freed.at[n], 1)
+        fold_copy(3 + n).start()
     exchange(m + 3)
-    for c in range(2):
-        fold_in(2 + c, c)
-        free(credit.at[c], cross)
-    for c in range(2):
-        pl.semaphore_wait(credit.at[c], 1)
-        cross_copy(1 + c).start()
-    pl.loop(0, chunks)(lambda c: fold_copy(c).wait_send())
+    for n in range(2):
+        fold_in(3 + n)
+        free(credit.at[n], cross)
+    for n in range(2):
+        pl.semaphore_wait(credit.at[n], 1)
+        cross_copy(2 + n).start()
+    for n in range(len(pieces)):
+        fold_copy(n).wait_send()
     free(freed.at[2], sib)
 
     def first_sums():
-        cross_copy(0).wait_recv()
-        acc[0, part_of(0), :] += tmp[2]
+        for n in range(2):
+            cross_copy(n).wait_recv()
+
+        @pl.loop(0, 2)
+        def _(i):
+            part = pl.ds(pl.multiple_of(i * h, h), h)
+            acc[0, part, :] += tmp[2, part, :]
+
         free(credit.at[2], cross)
 
     def last_sums():
         pl.semaphore_wait(credit.at[2], 1)
-        cross_copy(3).start()
+        cross_copy(4).start()
 
     run(m + 4, 5 * slots, 6, lambda q: triple(2, q, 0))
     row_copy(3, sib).wait_send()
@@ -312,10 +341,11 @@
     far_copy(0).wait_recv()
     pl.semaphore_wait(freed.at[2], 1)
 
-    @pl.loop(0, chunks)
-    def _(c):
-        work(held_index(last, 2), 1, [c * chunk], chunk)
-        last_copy(c).start()
+    @pl.loop(0, 2)
+    def _(q):
+        work(held_index(last, 2), 1, [(2 * q + n) * chunk for n in range(2)], chunk)
+        last_copy(2 * q).start()
+        last_copy(2 * q + 1).start()
 
     pl.loop(0, 3)(lambda q: unit(held_index(last, q), 0))
 
@@ -333,11 +363,12 @@
         gate_copy(k, where).wait_send()
     hid_again.wait()
 
+    for n in range(len(pieces)):
+        cross_copy(n).wait_send()
     for c in range(chunks):
         last_copy(c).wait()
-        cross_copy(c).wait_send()
         if c:
-            cross_copy(c).wait_recv()
+            cross_copy(c + 1).wait_recv()
 
         @pl.loop(0, chunk // nrm)
         def _(i):
@@ -372,7 +403,7 @@
         out = pl.pallas_call(
             functools.partial(moe_kernel, side, chips, excl),
             out_shape=pltpu.VMEM((tok, d_model), jnp.bfloat16),
-            in_specs=[any_space, vmem, vmem, vmem, vmem, any_space, any_space, any_space],
+            in_specs=[any_space, vmem, vmem, vmem, any_space, any_space, any_space, any_space],
             out_specs=vmem,
             scratch_shapes=[
                 pltpu.VMEM((held, chips, 3, shard, d_model), jnp.bfloat16),
@@ -382,9 +413,9 @@
                 pltpu.VMEM((tok, 4 * experts), jnp.float32),
                 pltpu.VMEM((3, tok // 4, d_model), jnp.float32),
                 dma((count + 1,)), dma((count + 1,)), dma((count,)), dma((count,)), dma((count,)), dma((count,)),
-                dma((10,)),
+                dma((11,)),
                 dma((3,)), dma((3,)), dma((3,)), dma((3,)),
-                dma((4,)), dma((4,)), dma((4,)), dma((4,)), dma((4,)), dma((4,)),
+                dma((5,)), dma((5,)), dma((5,)), dma((5,)), dma((4,)), dma((4,)),
                 pltpu.SemaphoreType.REGULAR((3,)), pltpu.SemaphoreType.REGULAR((3,)),
             ],
             compiler_params=pltpu.CompilerParams(collective_id=0, has_side_effects=True, vmem_limit_bytes=VMEM_BYTES - OUT),

time: 238 us -> 239 us (level)
  no operation moved by 1% of the time
where the time goes in v2:
time: 239 us; the launch traced here: 238 us
  Pallas kernels  238 us (100%)
    pallas_call x1, Pallas kernels, local_block(): pl.pallas_call(functools.partial(moe_kernel, side, chips, excl), out_shap...  237 us

profile of v2, /device:TPU:21, one launch (start us, length us, event | category | flops | bytes accessed | tf_op | source)
XLA Modules:
  0.0 238.2 jit_solution(17576516000715295407)
XLA Ops:
  0.0 236.7 %shard_map.82.src_ref = bf16[1024,1024]{1,0:T(8,128)(2,1)S(1)} custom-call(bf16[1024,1024]{1,0:T(8,128)(2,1)} %hid_ref.1, s32[8,1024]{1,0:T(8,128)} %bitcast.9, f32[1,1024]{1,0:T(1,128)} %bitcast.10, f32[1,1024]{1,0:T(1,128)} %bitcast.11, bf16[32,1024]{1,0:T(8,128)(2,1)} %bitcast.8, bf16[32,32,1024]{2,1,0:T(8,128)(2,1)} %bitcast.6, ...), custom_call_target="tpu_custom_call" | custom-call | flops 103079215104 | bytes 67108864 | tf_op jit(solution)/shard_map/pallas_call | solution.py:403
  236.7 1.3 shard_map.83

commit v3 on v1

--- a/solution.py
+++ b/solution.py
@@ -242,8 +242,8 @@
         gate_copy(3, sib).wait_recv()
         spread_gates(3)
 
-    run(2 * slots, 3 * slots, 12, lambda q: triple(1 - q // 6, q % 6, 2 * (q // 6)), [(2, lambda: partner_slices(1)), (4, far_rows)])
-    run(3 * slots, 4 * slots - 1, 12, lambda q: triple(1 + q // 6, q % 6, 2), [(5, lambda: partner_slices(2))])
+    run(2 * slots, 3 * slots, 12, lambda q: unit(held_index((q % 6) // 3, q % 3), 2 + q // 6), [(2, lambda: partner_slices(1)), (3, far_rows)])
+    run(3 * slots, 4 * slots - 1, 6, lambda q: triple(2, q, 2), [(4, lambda: partner_slices(2))])
     m = 4 * slots - 1
     exchange(m)
 
@@ -296,12 +296,15 @@
         pl.semaphore_wait(credit.at[2], 1)
         cross_copy(3).start()
 
-    run(m + 4, 5 * slots, 6, lambda q: triple(2, q, 0))
+    def own(q):
+        triple(1 + q // 6, q % 6, 0)
+
+    run(m + 4, 5 * slots, 7, own)
     row_copy(3, sib).wait_send()
     hid_again = pltpu.make_async_copy(hid_ref, rows.at[3], load_sem.at[9])
     hid_again.start()
-    run(5 * slots, 6 * slots, 12, lambda q: triple(3 + q // 6, q % 6, 0), [(4, first_sums), (5, lambda: partner_slices(4)), (6, last_sums)])
-    run(6 * slots, 7 * slots - 1, 6, lambda q: triple(5, q, 0), [(4, lambda: partner_slices(5))], more=False)
+    run(5 * slots, 6 * slots, 13, lambda q: own(7 + q), [(4, first_sums), (6, last_sums)])
+    run(6 * slots, 7 * slots - 1, 10, lambda q: own(20 + q), [(0, lambda: partner_slices(4)), (4, lambda: partner_slices(5))], more=False)
     last = rounds - 1
     partner_slices(last, 0, slots - 2)
     far_copy(1).start()

time: 238 us -> 238 us (level)
  no operation moved by 1% of the time
where the time goes in v3:
time: 238 us; the launch traced here: 237 us
  Pallas kernels  237 us (100%)
    pallas_call x1, Pallas kernels, local_block(): pl.pallas_call(functools.partial(moe_kernel, side, chips, excl), out_shap...  236 us

profile of v3, /device:TPU:21, one launch (start us, length us, event | category | flops | bytes accessed | tf_op | source)
XLA Modules:
  0.0 237.1 jit_solution(3798094907034663331)
XLA Ops:
  0.0 235.6 %shard_map.82.src_ref = bf16[1024,1024]{1,0:T(8,128)(2,1)S(1)} custom-call(bf16[1024,1024]{1,0:T(8,128)(2,1)} %hid_ref.1, s32[8,1024]{1,0:T(8,128)} %bitcast.9, f32[1,1024]{1,0:T(1,128)} %bitcast.10, f32[1,1024]{1,0:T(1,128)} %bitcast.11, bf16[32,1024]{1,0:T(8,128)(2,1)} %bitcast.8, bf16[32,32,1024]{2,1,0:T(8,128)(2,1)} %bitcast.6, ...), custom_call_target="tpu_custom_call" | custom-call | flops 103079215104 | bytes 67108864 | tf_op jit(solution)/shard_map/pallas_call | solution.py:375
  235.6 1.3 shard_map.83

commit v4 on v2

--- a/solution.py
+++ b/solution.py
@@ -129,7 +129,8 @@
         for k, src in enumerate((wg_ref, wl_ref, wd_ref)):
             loads.append(pltpu.make_async_copy(src.at[pl.ds(src0, size)], wts.at[pl.ds(dst0, size), z, k], load_sem.at[3 * n + k]))
     hid_load = pltpu.make_async_copy(hid_ref, rows.at[0], load_sem.at[9])
-    for load in loads[:3]:
+    router_load = pltpu.make_async_copy(router_ref, out_ref.at[pl.ds(0, experts)], load_sem.at[10])
+    for load in loads[:3] + [hid_load, router_load] + loads[3:]:
         load.start()
 
     barrier = pltpu.get_barrier_semaphore()
@@ -143,9 +144,6 @@
         up_copy(m, 1).start()
         dn_copy(m, 1).start()
 
-    router_load = pltpu.make_async_copy(router_ref, out_ref.at[pl.ds(0, experts)], load_sem.at[10])
-    for load in [hid_load, router_load] + loads[3:]:
-        load.start()
     nrm = min(128, chunk)
 
     @pl.loop(0, 4 * tok // nrm)
@@ -291,6 +289,8 @@
     fold_in(2)
     free(freed.at[1], sib)
 
+    exchange(m + 3)
+
     @pl.loop(2, chunks)
     def _(c):
         late(3, c * chunk, chunk)
@@ -299,10 +299,11 @@
     for n in range(2):
         pl.semaphore_wait(freed.at[n], 1)
         fold_copy(3 + n).start()
-    exchange(m + 3)
+    exchange(m + 4)
     for n in range(2):
         fold_in(3 + n)
         free(credit.at[n], cross)
+    exchange(m + 5)
     for n in range(2):
         pl.semaphore_wait(credit.at[n], 1)
         cross_copy(2 + n).start()
@@ -325,12 +326,15 @@
         pl.semaphore_wait(credit.at[2], 1)
         cross_copy(4).start()
 
-    run(m + 4, 5 * slots, 6, lambda q: triple(2, q, 0))
+    def own(q):
+        triple(2 + q // 6, q % 6, 0)
+
+    run(m + 6, 5 * slots, 3, own)
     row_copy(3, sib).wait_send()
     hid_again = pltpu.make_async_copy(hid_ref, rows.at[3], load_sem.at[9])
     hid_again.start()
-    run(5 * slots, 6 * slots, 12, lambda q: triple(3 + q // 6, q % 6, 0), [(4, first_sums), (5, lambda: partner_slices(4)), (6, last_sums)])
-    run(6 * slots, 7 * slots - 1, 6, lambda q: triple(5, q, 0), [(4, lambda: partner_slices(5))], more=False)
+    run(5 * slots, 6 * slots, 12, lambda q: own(3 + q), [(4, first_sums), (6, last_sums)])
+    run(6 * slots, 7 * slots - 1, 9, lambda q: own(15 + q), [(0, lambda: partner_slices(4)), (4, lambda: partner_slices(5))], more=False)
     last = rounds - 1
     partner_slices(last, 0, slots - 2)
     far_copy(1).start()

time: 239 us -> 237 us (level)
  no operation moved by 1% of the time
where the time goes in v4:
time: 237 us; the launch traced here: 236 us
  Pallas kernels  236 us (100%)
    pallas_call x1, Pallas kernels, local_block(): pl.pallas_call(functools.partial(moe_kernel, side, chips, excl), out_shap...  234 us

profile of v4, /device:TPU:21, one launch (start us, length us, event | category | flops | bytes accessed | tf_op | source)
XLA Modules:
  0.0 235.8 jit_solution(7338653399278683967)
XLA Ops:
  0.0 234.3 %shard_map.82.src_ref = bf16[1024,1024]{1,0:T(8,128)(2,1)S(1)} custom-call(bf16[1024,1024]{1,0:T(8,128)(2,1)} %hid_ref.1, s32[8,1024]{1,0:T(8,128)} %bitcast.9, f32[1,1024]{1,0:T(1,128)} %bitcast.10, f32[1,1024]{1,0:T(1,128)} %bitcast.11, bf16[32,1024]{1,0:T(8,128)(2,1)} %bitcast.8, bf16[32,32,1024]{2,1,0:T(8,128)(2,1)} %bitcast.6, ...), custom_call_target="tpu_custom_call" | custom-call | flops 103079215104 | bytes 67108864 | tf_op jit(solution)/shard_map/pallas_call | solution.py:407
  234.3 1.3 shard_map.83

commit v5 on v4

--- a/solution.py
+++ b/solution.py
@@ -107,7 +107,8 @@
         return pl.ds(pl.multiple_of(c * chunk, chunk), chunk)
 
     h = chunk // 2
-    pieces = ((0, h, 0, 0, 2, 0), (h, h, 0, h, 2, h), (chunk, chunk, 1, 0, 0, 0), (2 * chunk, chunk, 0, 0, 1, 0), (3 * chunk, chunk, 1, 0, 2, 0))
+    g = h // 2
+    pieces = ((0, g, 0, 0, 2, 0), (g, g, 0, g, 2, g), (h, h, 0, h, 2, h), (chunk, chunk, 1, 0, 0, 0), (2 * chunk, chunk, 0, 0, 1, 0), (3 * chunk, chunk, 1, 0, 2, 0))
 
     def fold_copy(n):
         at, size, slot, row, _, _ = pieces[n]
@@ -266,29 +267,35 @@
         at, size, slot, row, _, _ = pieces[n]
         fold_copy(n).wait_recv()
 
-        @pl.loop(0, size // h)
+        step = min(size, h)
+
+        @pl.loop(0, size // step)
         def _(i):
-            acc[2, pl.ds(pl.multiple_of(at + i * h, h), h), :] += tmp[slot, pl.ds(pl.multiple_of(row + i * h, h), h), :]
+            acc[2, pl.ds(pl.multiple_of(at + i * step, step), step), :] += tmp[slot, pl.ds(pl.multiple_of(row + i * step, step), step), :]
 
     @pl.loop(0, 2)
     def _(n):
-        late(3, n * h, h)
-        part = pl.ds(pl.multiple_of(n * h, h), h)
+        late(3, n * g, g)
+        part = pl.ds(pl.multiple_of(n * g, g), g)
         remote(acc.at[3, part], tmp.at[0, part], fold_ss.at[n], fold_rs.at[n], sib).start()
-        late(2, n * h, h)
+        late(2, n * g, g)
 
     late(3, *pieces[2][:2])
     fold_copy(2).start()
     fold_in(0)
     cross_copy(0).start()
+    late(2, *pieces[2][:2])
     exchange(m + 2)
-    late(2, *pieces[2][:2])
     fold_in(1)
     cross_copy(1).start()
+    late(3, *pieces[3][:2])
+    fold_copy(3).start()
+    fold_in(2)
+    cross_copy(2).start()
     free(freed.at[0], sib)
-    fold_in(2)
+    late(2, *pieces[3][:2])
+    fold_in(3)
     free(freed.at[1], sib)
-
     exchange(m + 3)
 
     @pl.loop(2, chunks)
@@ -298,21 +305,21 @@
 
     for n in range(2):
         pl.semaphore_wait(freed.at[n], 1)
-        fold_copy(3 + n).start()
+        fold_copy(4 + n).start()
     exchange(m + 4)
     for n in range(2):
-        fold_in(3 + n)
+        fold_in(4 + n)
         free(credit.at[n], cross)
     exchange(m + 5)
     for n in range(2):
         pl.semaphore_wait(credit.at[n], 1)
-        cross_copy(2 + n).start()
+        cross_copy(3 + n).start()
     for n in range(len(pieces)):
         fold_copy(n).wait_send()
     free(freed.at[2], sib)
 
     def first_sums():
-        for n in range(2):
+        for n in range(3):
             cross_copy(n).wait_recv()
 
         @pl.loop(0, 2)
@@ -324,7 +331,7 @@
 
     def last_sums():
         pl.semaphore_wait(credit.at[2], 1)
-        cross_copy(4).start()
+        cross_copy(5).start()
 
     def own(q):
         triple(2 + q // 6, q % 6, 0)
@@ -372,7 +379,7 @@
     for c in range(chunks):
         last_copy(c).wait()
         if c:
-            cross_copy(c + 1).wait_recv()
+            cross_copy(c + 2).wait_recv()
 
         @pl.loop(0, chunk // nrm)
         def _(i):
@@ -419,7 +426,7 @@
                 dma((count + 1,)), dma((count + 1,)), dma((count,)), dma((count,)), dma((count,)), dma((count,)),
                 dma((11,)),
                 dma((3,)), dma((3,)), dma((3,)), dma((3,)),
-                dma((5,)), dma((5,)), dma((5,)), dma((5,)), dma((4,)), dma((4,)),
+                dma((6,)), dma((6,)), dma((6,)), dma((6,)), dma((4,)), dma((4,)),
                 pltpu.SemaphoreType.REGULAR((3,)), pltpu.SemaphoreType.REGULAR((3,)),
             ],
             compiler_params=pltpu.CompilerParams(collective_id=0, has_side_effects=True, vmem_limit_bytes=VMEM_BYTES - OUT),

time: 237 us -> 238 us (level)
  no operation moved by 1% of the time
where the time goes in v5:
time: 238 us; the launch traced here: 237 us
  Pallas kernels  237 us (100%)
    pallas_call x1, Pallas kernels, local_block(): pl.pallas_call(functools.partial(moe_kernel, side, chips, excl), out_shap...  235 us

profile of v5, /device:TPU:21, one launch (start us, length us, event | category | flops | bytes accessed | tf_op | source)
XLA Modules:
  0.0 236.8 jit_solution(17644148890767012630)
XLA Ops:
  0.0 235.3 %shard_map.82.src_ref = bf16[1024,1024]{1,0:T(8,128)(2,1)S(1)} custom-call(bf16[1024,1024]{1,0:T(8,128)(2,1)} %hid_ref.1, s32[8,1024]{1,0:T(8,128)} %bitcast.9, f32[1,1024]{1,0:T(1,128)} %bitcast.10, f32[1,1024]{1,0:T(1,128)} %bitcast.11, bf16[32,1024]{1,0:T(8,128)(2,1)} %bitcast.8, bf16[32,32,1024]{2,1,0:T(8,128)(2,1)} %bitcast.6, ...), custom_call_target="tpu_custom_call" | custom-call | flops 103079215104 | bytes 67108864 | tf_op jit(solution)/shard_map/pallas_call | solution.py:414
  235.3 1.3 shard_map.83

commit v6 on v4

--- a/solution.py
+++ b/solution.py
@@ -257,7 +257,7 @@
 
     pl.loop(0, 2)(lambda q: unit(excl - 1, 3 - q))
     exchange(m + 1)
-    partner_slices(3)
+    pl.when(py == 1)(lambda: partner_slices(3))
 
     def late(k, start, size):
         work(excl - 2, k, [start], size)
@@ -333,7 +333,7 @@
     row_copy(3, sib).wait_send()
     hid_again = pltpu.make_async_copy(hid_ref, rows.at[3], load_sem.at[9])
     hid_again.start()
-    run(5 * slots, 6 * slots, 12, lambda q: own(3 + q), [(4, first_sums), (6, last_sums)])
+    run(5 * slots, 6 * slots, 12, lambda q: own(3 + q), [(0, lambda: pl.when(py == 0)(lambda: partner_slices(3))), (4, first_sums), (6, last_sums)])
     run(6 * slots, 7 * slots - 1, 9, lambda q: own(15 + q), [(0, lambda: partner_slices(4)), (4, lambda: partner_slices(5))], more=False)
     last = rounds - 1
     partner_slices(last, 0, slots - 2)

time: 237 us -> 237 us (level)
  no operation moved by 1% of the time
where the time goes in v6:
time: 237 us; the launch traced here: 236 us
  Pallas kernels  236 us (100%)
    pallas_call x1, Pallas kernels, local_block(): pl.pallas_call(functools.partial(moe_kernel, side, chips, excl), out_shap...  235 us

profile of v6, /device:TPU:21, one launch (start us, length us, event | category | flops | bytes accessed | tf_op | source)
XLA Modules:
  0.0 236.3 jit_solution(3026201526896188914)
XLA Ops:
  0.0 234.7 %shard_map.82.src_ref = bf16[1024,1024]{1,0:T(8,128)(2,1)S(1)} custom-call(bf16[1024,1024]{1,0:T(8,128)(2,1)} %hid_ref.1, s32[8,1024]{1,0:T(8,128)} %bitcast.9, f32[1,1024]{1,0:T(1,128)} %bitcast.10, f32[1,1024]{1,0:T(1,128)} %bitcast.11, bf16[32,1024]{1,0:T(8,128)(2,1)} %bitcast.8, bf16[32,32,1024]{2,1,0:T(8,128)(2,1)} %bitcast.6, ...), custom_call_target="tpu_custom_call" | custom-call | flops 103079215104 | bytes 67108864 | tf_op jit(solution)/shard_map/pallas_call | solution.py:407
  234.7 1.3 shard_map.83

commit v7 on v4

--- a/solution.py
+++ b/solution.py
@@ -81,13 +81,16 @@
             up_copy(m + 2, 1).start()
         else:
             pl.when(m + 2 < count)(lambda: up_copy(m + 2, 1).start())
+        odd = (m % slots) % 2
+        if along_y:
+            pl.when(odd == 0)(lambda: y_copy(m, 2 * py).start())
         dn_copy(m, 0).wait_recv()
         if more is True:
             dn_copy(m + 2, 1).start()
         else:
             pl.when(m + 2 < count)(lambda: dn_copy(m + 2, 1).start())
         if along_y:
-            y_copy(m, 2 * py).start()
+            pl.when(odd == 1)(lambda: y_copy(m, 2 * py).start())
 
     def partner_slices(r, first=0, end=slots):
         @pl.loop(first, end)

time: 237 us -> 237 us (level)
  no operation moved by 1% of the time
where the time goes in v7:
time: 237 us; the launch traced here: 236 us
  Pallas kernels  236 us (100%)
    pallas_call x1, Pallas kernels, local_block(): pl.pallas_call(functools.partial(moe_kernel, side, chips, excl), out_shap...  234 us

profile of v7, /device:TPU:21, one launch (start us, length us, event | category | flops | bytes accessed | tf_op | source)
XLA Modules:
  0.0 235.9 jit_solution(3217014509142142117)
XLA Ops:
  0.0 234.4 %shard_map.82.src_ref = bf16[1024,1024]{1,0:T(8,128)(2,1)S(1)} custom-call(bf16[1024,1024]{1,0:T(8,128)(2,1)} %hid_ref.1, s32[8,1024]{1,0:T(8,128)} %bitcast.9, f32[1,1024]{1,0:T(1,128)} %bitcast.10, f32[1,1024]{1,0:T(1,128)} %bitcast.11, bf16[32,1024]{1,0:T(8,128)(2,1)} %bitcast.8, bf16[32,32,1024]{2,1,0:T(8,128)(2,1)} %bitcast.6, ...), custom_call_target="tpu_custom_call" | custom-call | flops 103079215104 | bytes 67108864 | tf_op jit(solution)/shard_map/pallas_call | solution.py:410
  234.4 1.3 shard_map.83
